TPU v7x, 256 devices: a whole 4x4x8 slice. The times are simulated.
256 devices in a mesh: dp: 64 (over y, z, core), neg: 4 (over x).
Axes of the slice: x: 4, y: 4, z: 8, core: 2. Of those that a mesh axis runs over, the one named last changes fastest.
Arguments:
- user_embed: bfloat16 [196608, 256], P(('dp', 'neg')), may hold values from -25 to 25
- positive_embed: bfloat16 [196608, 256], P(('dp', 'neg')), may hold values from -6 to 6
- positive_ids: int32 [196608], P(('dp', 'neg')), may hold values from 0 to 1048575
- token_weights: int32 [196608], P(('dp', 'neg')), may hold values from 1 to 5
- offsets: int32 [64, 25], P('dp'), may hold values from 0 to 3072, as said below
- negative_embed: bfloat16 [32768, 256], P('neg'), may hold values from -6 to 6
- negative_ids: int32 [32768], P('neg'), may hold values from 0 to 1048575
Outputs:
- token_loss: float32 [196608], P(('dp', 'neg'))
- mean_loss: float32 [], replicated
Inputs may be any that keep to these rules, and one draw needn't show every extreme that they name: `offsets`: each row starts at 0 and does not fall; every user holds 2 or more slots; in every draw some group fills all 3072 slots.
All inputs are finite; a program needn't handle non-finite values.
Results may differ from a plain program's by a relative error of at most 0.0003.
Values may be sent and summed in bfloat16 or wider, within the bound.
A program may use at most 64 MiB of HBM per device.

v0:
```python
import functools
import math

import jax
import jax.numpy as jnp
from jax import lax
from jax.sharding import Mesh
from jax.sharding import PartitionSpec as P

DP_NEG = ("dp_0", "dp_1", "dp_2", "neg")
DP = ("dp_0", "dp_1", "dp_2")


floor_value = -1e30


def copy_for_each(array, axis):
    peers = lax.axis_size(axis)
    return lax.all_to_all(
        jnp.broadcast_to(array[None], (peers, *array.shape)), axis, 0, 0, tiled=True
    )


def laid_out(pieces, dim):
    pieces = jnp.moveaxis(pieces, 0, dim)
    lengths = pieces.shape
    return pieces.reshape(*lengths[:dim], lengths[dim] * lengths[dim + 1], *lengths[dim + 2 :])


def collect(array, axis, dim):
    pieces = copy_for_each(array, axis)
    return laid_out(pieces, dim)


def all_in_one(array, axis):
    leaves = jax.tree.leaves(array)
    sequence = sorted(range(len(leaves)), key=lambda k: -leaves[k].size)
    width = (1, *leaves[sequence[0]].shape)[-1]
    lines = [
        jnp.pad(leaves[k].reshape(-1), (0, -leaves[k].size % width)).reshape(-1, width)
        for k in sequence
    ]
    both, at, found = (copy_for_each(jnp.concatenate(lines), axis), 0, {})
    for k, line in zip(sequence, lines):
        share = both[:, at : at + len(line)].reshape(len(both), -1)
        found[k] = share[:, : leaves[k].size].reshape(-1, *leaves[k].shape)
        at += len(line)
    numbers = iter(range(len(leaves)))
    return jax.tree.map(lambda _: found[next(numbers)], array)


def joined_by_halves(pieces, combine):
    while len(jax.tree.leaves(pieces)[0]) > 1:
        pieces = jax.vmap(combine)(
            *(jax.tree.map(lambda part: part[side::2], pieces) for side in (0, 1))
        )
    return jax.tree.map(lambda part: part[0], pieces)


def combined_all(array, axis, combine):
    pieces = all_in_one(array, axis)
    return joined_by_halves(pieces, combine)


def one_axis_at_a_time(array, axes):
    return functools.reduce(lax.psum, axes, array)


def shard_partials(rows, row_ids, columns, column_ids, scale):
    logits = (
        lax.dot_general(rows, columns, (((1,), (1,)), ((), ())), preferred_element_type=jnp.float32)
        * scale
    )
    hit = row_ids[:, None] == column_ids[None, :]
    peak = jnp.max(jnp.where(hit, floor_value, logits), axis=1)
    summed = jnp.sum(jnp.where(hit, 0.0, jnp.exp(logits - peak[:, None])), axis=1)
    return (peak, summed)


def combine(first, second):
    peak = jnp.maximum(first[0], second[0])
    return (peak, first[1] * jnp.exp(first[0] - peak) + second[1] * jnp.exp(second[0] - peak))


def shards(
    user_embed, positive_embed, positive_ids, token_weights, offsets, negative_embed, negative_ids
):
    tok_rows = user_embed.shape[0]
    width = user_embed.shape[1]
    scale = 3.0 / math.sqrt(width)
    positions = lax.axis_index("neg") * tok_rows + jnp.arange(tok_rows, dtype=jnp.int32)
    ends = offsets[0, 1:]
    last_slot = jnp.any(positions[:, None] + 1 == ends[None, :], axis=1)
    live = (positions < offsets[0, -1]) & jnp.logical_not(last_slot)
    weight = token_weights.astype(jnp.float32)
    live_weight = weight * live.astype(jnp.float32)
    rows = collect(user_embed, "neg", 0)
    row_ids = collect(positive_ids, "neg", 0)
    number = rows.shape[0]
    block = math.gcd(number, 512)
    blocks = rows.reshape(number // block, block, width)
    id_blocks = row_ids.reshape(number // block, block)

    def one_block(pair):
        return shard_partials(pair[0], pair[1], negative_embed, negative_ids, scale)

    peaks, sums = lax.map(one_block, (blocks, id_blocks))
    new_peaks = peaks.reshape(number)
    new_sums = sums.reshape(number)
    peaks = new_peaks
    sums = new_sums
    peaks, sums = combined_all((peaks, sums), "neg", combine)
    own_start = lax.axis_index("neg") * tok_rows
    peaks = lax.dynamic_slice_in_dim(peaks, own_start, tok_rows, 0)
    sums = lax.dynamic_slice_in_dim(sums, own_start, tok_rows, 0)
    positive = (
        jnp.sum(user_embed.astype(jnp.float32) * positive_embed.astype(jnp.float32), axis=1) * scale
    )
    top = jnp.maximum(peaks, positive)
    lse = top + jnp.log(sums * jnp.exp(peaks - top) + jnp.exp(positive - top))
    token_loss = jnp.where(live, lse - positive, 0.0).astype(jnp.float32)
    weighted = jnp.sum(weight * token_loss)
    total, count = (
        one_axis_at_a_time(weighted, DP_NEG),
        one_axis_at_a_time(jnp.sum(live_weight), DP_NEG),
    )
    return (token_loss, total / count)


def solution(mesh):
    split = Mesh(mesh.devices.reshape(4, 8, 2, mesh.shape["neg"]), ("dp_0", "dp_1", "dp_2", "neg"))
    return jax.shard_map(
        shards,
        mesh=split,
        in_specs=(
            P(DP_NEG, None),
            P(DP_NEG, None),
            P(DP_NEG),
            P(DP_NEG),
            P(DP, None),
            P("neg", None),
            P("neg"),
        ),
        out_specs=(P(DP_NEG), P()),
        check_vma=False,
    )
```

profile of v0, /device:TPU:1, one launch (start us, length us, event | category | flops | bytes accessed | tf_op | source)
XLA Modules:
  0.0 154.0 jit_solution(10713202898961529094)
XLA Ops:
  0.6 0.7 broadcast_in_dim.40
  1.3 8.8 %all_to_all.16 = s32[4,1,768]{2,1,0:T(1,128)S(1)} all-to-all(s32[4,1,768]{2,1,0:T(1,128)S(1)} %broadcast_in_dim.40), channel_id=1, replica_groups=mesh['dp_0'=4,'dp_1'=8,'dp_2'=2,'neg'=4] {'neg'}, dimensions={0} | all-to-all | bytes 24576 | tf_op jit(solution)/shard_map/all_to_all | solution.py:19
  10.1 2.2 %broadcast_in_dim.41 = bf16[4,768,256]{2,1,0:T(8,128)(2,1)} broadcast(bf16[768,256]{1,0:T(8,128)(2,1)} %param.9), dimensions={1,2} | broadcast | bytes 1966080 | tf_op jit(solution)/shard_map/broadcast_in_dim | solution.py:20
  12.4 3.6 %all-to-all-start.1 = ((bf16[4,768,256]{2,1,0:T(8,128)(2,1)}), bf16[4,768,256]{2,1,0:T(8,128)(2,1)S(1)}, u32[]{:S(2)}, u32[]{:S(2)}) async-start(bf16[4,768,256]{2,1,0:T(8,128)(2,1)} %broadcast_in_dim.41), calls=%async_computation.1 | async-start | bytes 3145728 | tf_op jit(solution)/shard_map/all_to_all | solution.py:19
  16.0 1.2 slice.40
  17.2 1.3 multiply_reduce_fusion
  18.5 0.7 slice_bitcast_fusion
  19.3 15.3 %all-to-all-done.1 = bf16[4,768,256]{2,1,0:T(8,128)(2,1)S(1)} async-done(((bf16[4,768,256]{2,1,0:T(8,128)(2,1)}), bf16[4,768,256]{2,1,0:T(8,128)(2,1)S(1)}, u32[]{:S(2)}, u32[]{:S(2)}) %all-to-all-start.1) | async-done | bytes 1572896 | tf_op jit(solution)/shard_map/all_to_all | solution.py:19
  34.6 0.0 copy-start.1
  34.6 59.5 %while.12 = (s32[]{:T(128)}, f32[6,512]{1,0:T(8,128)S(1)}, f32[6,512]{1,0:T(8,128)S(1)}, s32[6,512]{1,0:T(8,128)S(1)}, s32[8192]{0:T(1024)}, /*index=5*/bf16[6,5...) while((s32[]{:T(128)}, f32[6,512]{1,0:T(8,128)S(1)}, f32[6,512]{1,0:T(8,128)S(1)}, ...), condition=%wide.region_4.5_spmd, body=%wide.region_1.4_spmd.sunk | while | flops 2185231360 | bytes 38230152 | solution.py:107
  34.6 0.0 copy-start
  34.6 5.1 %fusion.22 = (f32[512]{0:T(512)S(1)}, f32[512,8192]{1,0:T(8,128)S(1)}) fusion(s32[8192]{0:T(1024)} %get-tuple-element.151, s32[512]{0:T(512)S(1)} %bitcast.35, bf16[8192,256]{1,0:T(8,128)(2,1)} %get-tuple-element.153, bf16[6,512,256]{2,1,0:T(8,128)(2,1)S(1)} %get-tuple-element.152, s32[]{:T(128)} %get-tuple-element.138), kind=kOutput, calls=%fused_computation.2.clone.1 | convolution fusion | flops 2164260352 | bytes 21270532 | tf_op jit(solution)/shard_map/while/body/eval_jaxpr/dot_general | solution.py:71
  39.7 0.0 copy-done
  39.7 4.6 %fusion.23 = f32[512]{0:T(512)S(1)} fusion(f32[512,8192]{1,0:T(8,128)S(1)} %get-tuple-element.128, f32[512]{0:T(512)S(1)} %get-tuple-element.127, s32[8192]{0:T(1024)S(1)} %copy-done, s32[512]{0:T(512)S(1)} %bitcast.36), kind=kLoop, calls=%fused_computation.3.clone.1 | loop fusion | flops 20971008 | bytes 16816128 | tf_op jit(solution)/shard_map/while/body/eval_jaxpr/reduce_sum | solution.py:76
  44.4 0.1 dynamic_update_slice.10
  44.5 0.1 dynamic_update_slice.9
  44.5 0.0 copy-start
  44.6 5.1 %fusion.22 = (f32[512]{0:T(512)S(1)}, f32[512,8192]{1,0:T(8,128)S(1)}) fusion(s32[8192]{0:T(1024)} %get-tuple-element.151, s32[512]{0:T(512)S(1)} %bitcast.35, bf16[8192,256]{1,0:T(8,128)(2,1)} %get-tuple-element.153, bf16[6,512,256]{2,1,0:T(8,128)(2,1)S(1)} %get-tuple-element.152, s32[]{:T(128)} %get-tuple-element.138), kind=kOutput, calls=%fused_computation.2.clone.1 | convolution fusion | flops 2164260352 | bytes 21270532 | tf_op jit(solution)/shard_map/while/body/eval_jaxpr/dot_general | solution.py:71
  49.7 0.0 copy-done
  49.7 4.6 %fusion.23 = f32[512]{0:T(512)S(1)} fusion(f32[512,8192]{1,0:T(8,128)S(1)} %get-tuple-element.128, f32[512]{0:T(512)S(1)} %get-tuple-element.127, s32[8192]{0:T(1024)S(1)} %copy-done, s32[512]{0:T(512)S(1)} %bitcast.36), kind=kLoop, calls=%fused_computation.3.clone.1 | loop fusion | flops 20971008 | bytes 16816128 | tf_op jit(solution)/shard_map/while/body/eval_jaxpr/reduce_sum | solution.py:76
  54.3 0.1 dynamic_update_slice.10
  54.4 0.1 dynamic_update_slice.9
  54.5 0.0 copy-start
  54.5 5.1 %fusion.22 = (f32[512]{0:T(512)S(1)}, f32[512,8192]{1,0:T(8,128)S(1)}) fusion(s32[8192]{0:T(1024)} %get-tuple-element.151, s32[512]{0:T(512)S(1)} %bitcast.35, bf16[8192,256]{1,0:T(8,128)(2,1)} %get-tuple-element.153, bf16[6,512,256]{2,1,0:T(8,128)(2,1)S(1)} %get-tuple-element.152, s32[]{:T(128)} %get-tuple-element.138), kind=kOutput, calls=%fused_computation.2.clone.1 | convolution fusion | flops 2164260352 | bytes 21270532 | tf_op jit(solution)/shard_map/while/body/eval_jaxpr/dot_general | solution.py:71
  59.6 0.0 copy-done
  59.6 4.6 %fusion.23 = f32[512]{0:T(512)S(1)} fusion(f32[512,8192]{1,0:T(8,128)S(1)} %get-tuple-element.128, f32[512]{0:T(512)S(1)} %get-tuple-element.127, s32[8192]{0:T(1024)S(1)} %copy-done, s32[512]{0:T(512)S(1)} %bitcast.36), kind=kLoop, calls=%fused_computation.3.clone.1 | loop fusion | flops 20971008 | bytes 16816128 | tf_op jit(solution)/shard_map/while/body/eval_jaxpr/reduce_sum | solution.py:76
  64.2 0.1 dynamic_update_slice.10
  64.3 0.1 dynamic_update_slice.9
  64.4 0.0 copy-start
  64.4 5.1 %fusion.22 = (f32[512]{0:T(512)S(1)}, f32[512,8192]{1,0:T(8,128)S(1)}) fusion(s32[8192]{0:T(1024)} %get-tuple-element.151, s32[512]{0:T(512)S(1)} %bitcast.35, bf16[8192,256]{1,0:T(8,128)(2,1)} %get-tuple-element.153, bf16[6,512,256]{2,1,0:T(8,128)(2,1)S(1)} %get-tuple-element.152, s32[]{:T(128)} %get-tuple-element.138), kind=kOutput, calls=%fused_computation.2.clone.1 | convolution fusion | flops 2164260352 | bytes 21270532 | tf_op jit(solution)/shard_map/while/body/eval_jaxpr/dot_general | solution.py:71
  69.5 0.0 copy-done
  69.5 4.6 %fusion.23 = f32[512]{0:T(512)S(1)} fusion(f32[512,8192]{1,0:T(8,128)S(1)} %get-tuple-element.128, f32[512]{0:T(512)S(1)} %get-tuple-element.127, s32[8192]{0:T(1024)S(1)} %copy-done, s32[512]{0:T(512)S(1)} %bitcast.36), kind=kLoop, calls=%fused_computation.3.clone.1 | loop fusion | flops 20971008 | bytes 16816128 | tf_op jit(solution)/shard_map/while/body/eval_jaxpr/reduce_sum | solution.py:76
  74.1 0.1 dynamic_update_slice.10
  74.2 0.1 dynamic_update_slice.9
  74.3 0.0 copy-start
  74.3 5.1 %fusion.22 = (f32[512]{0:T(512)S(1)}, f32[512,8192]{1,0:T(8,128)S(1)}) fusion(s32[8192]{0:T(1024)} %get-tuple-element.151, s32[512]{0:T(512)S(1)} %bitcast.35, bf16[8192,256]{1,0:T(8,128)(2,1)} %get-tuple-element.153, bf16[6,512,256]{2,1,0:T(8,128)(2,1)S(1)} %get-tuple-element.152, s32[]{:T(128)} %get-tuple-element.138), kind=kOutput, calls=%fused_computation.2.clone.1 | convolution fusion | flops 2164260352 | bytes 21270532 | tf_op jit(solution)/shard_map/while/body/eval_jaxpr/dot_general | solution.py:71
  79.4 0.0 copy-done
  79.4 4.6 %fusion.23 = f32[512]{0:T(512)S(1)} fusion(f32[512,8192]{1,0:T(8,128)S(1)} %get-tuple-element.128, f32[512]{0:T(512)S(1)} %get-tuple-element.127, s32[8192]{0:T(1024)S(1)} %copy-done, s32[512]{0:T(512)S(1)} %bitcast.36), kind=kLoop, calls=%fused_computation.3.clone.1 | loop fusion | flops 20971008 | bytes 16816128 | tf_op jit(solution)/shard_map/while/body/eval_jaxpr/reduce_sum | solution.py:76
  84.1 0.1 dynamic_update_slice.10
  84.1 0.1 dynamic_update_slice.9
  84.2 0.0 copy-start
  84.2 5.1 %fusion.22 = (f32[512]{0:T(512)S(1)}, f32[512,8192]{1,0:T(8,128)S(1)}) fusion(s32[8192]{0:T(1024)} %get-tuple-element.151, s32[512]{0:T(512)S(1)} %bitcast.35, bf16[8192,256]{1,0:T(8,128)(2,1)} %get-tuple-element.153, bf16[6,512,256]{2,1,0:T(8,128)(2,1)S(1)} %get-tuple-element.152, s32[]{:T(128)} %get-tuple-element.138), kind=kOutput, calls=%fused_computation.2.clone.1 | convolution fusion | flops 2164260352 | bytes 21270532 | tf_op jit(solution)/shard_map/while/body/eval_jaxpr/dot_general | solution.py:71
  89.3 0.0 copy-done
  89.3 4.6 %fusion.23 = f32[512]{0:T(512)S(1)} fusion(f32[512,8192]{1,0:T(8,128)S(1)} %get-tuple-element.128, f32[512]{0:T(512)S(1)} %get-tuple-element.127, s32[8192]{0:T(1024)S(1)} %copy-done, s32[512]{0:T(512)S(1)} %bitcast.36), kind=kLoop, calls=%fused_computation.3.clone.1 | loop fusion | flops 20971008 | bytes 16816128 | tf_op jit(solution)/shard_map/while/body/eval_jaxpr/reduce_sum | solution.py:76
  94.0 0.1 dynamic_update_slice.10
  94.1 0.1 dynamic_update_slice.9
  94.2 0.6 broadcast_in_dim.42
  94.9 3.3 %all-to-all-start.2 = ((f32[4,2,3072]{2,1,0:T(2,128)}), f32[4,2,3072]{2,1,0:T(2,128)S(1)}, u32[]{:S(2)}, u32[]{:S(2)}) async-start(f32[4,2,3072]{2,1,0:T(2,128)} %broadcast_in_dim.42), calls=%async_computation.2 | async-start | bytes 196608 | tf_op jit(solution)/shard_map/all_to_all | solution.py:19
  98.2 0.1 compare_reduce_fusion
  98.3 4.5 %all-to-all-done.2 = f32[4,2,3072]{2,1,0:T(2,128)S(1)} async-done(((f32[4,2,3072]{2,1,0:T(2,128)}), f32[4,2,3072]{2,1,0:T(2,128)S(1)}, u32[]{:S(2)}, u32[]{:S(2)}) %all-to-all-start.2) | async-done | bytes 98336 | tf_op jit(solution)/shard_map/all_to_all | solution.py:19
  102.8 0.1 fusion.15
  103.2 0.0 copy-done.1
  103.2 1.9 %select_reduce_fusion = (f32[]{:T(128)}, f32[]{:T(128)}, f32[768]{0:T(1024)}) fusion(s32[768]{0:T(1024)S(1)} %copy-done.1, pred[768]{0:T(1024)(128)(4,1)S(1)} %compare_reduce_fusion, s32[]{:T(128)} %bitcast.4, s32[]{:T(128)S(6)} %mul.37, f32[768]{0:T(1024)S(1)} %get-tuple-element.42, f32[768]{0:T(1024)S(1)} %get-tuple-element.43, f32[768]{0:T(1024)S(1)} %multiply_reduce_fusion), kind=kLoop, calls=%fused_computation.15 | loop fusion | flops 13822 | bytes 16144 | tf_op jit(solution)/shard_map/reduce_sum | solution.py:125
  105.1 9.4 %all-reduce.2 = (f32[]{:T(128)}, f32[]{:T(128)}) all-reduce(f32[]{:T(128)} %get-tuple-element.45, f32[]{:T(128)} %get-tuple-element.44), channel_id=1, replica_groups=mesh['dp_0'=4,'dp_1'=8,'dp_2'=2,'neg'=4] {'dp_0'}, use_global_device_ids=true, to_apply=%region_7.8 | all-reduce | flops 2 | bytes 16 | tf_op jit(solution)/shard_map/psum | solution.py:66
  114.5 16.9 %all-reduce = (f32[]{:T(128)}, f32[]{:T(128)}) all-reduce(f32[]{:T(128)} %get-tuple-element.64, f32[]{:T(128)} %get-tuple-element.65), channel_id=1, replica_groups=mesh['dp_0'=4,'dp_1'=8,'dp_2'=2,'neg'=4] {'dp_1'}, use_global_device_ids=true, to_apply=%region_8.9 | all-reduce | flops 2 | bytes 16 | tf_op jit(solution)/shard_map/psum | solution.py:66
  131.5 12.7 %all-reduce.3 = (f32[]{:T(128)}, f32[]{:T(128)}) all-reduce(f32[]{:T(128)} %get-tuple-element.60, f32[]{:T(128)} %get-tuple-element.61), channel_id=1, replica_groups=mesh['dp_0'=4,'dp_1'=8,'dp_2'=2,'neg'=4] {'dp_2'}, use_global_device_ids=true, to_apply=%region_9.10 | all-reduce | flops 2 | bytes 16 | tf_op jit(solution)/shard_map/psum | solution.py:66
  144.1 7.5 %all-reduce.1 = (f32[]{:T(128)}, f32[]{:T(128)}) all-reduce(f32[]{:T(128)} %get-tuple-element.66, f32[]{:T(128)} %get-tuple-element.67), channel_id=1, replica_groups=mesh['dp_0'=4,'dp_1'=8,'dp_2'=2,'neg'=4] {'neg'}, use_global_device_ids=true, to_apply=%region_10.11 | all-reduce | flops 2 | bytes 16 | tf_op jit(solution)/shard_map/psum | solution.py:66
  (23 shorter events, 0.5 us)
Async XLA Ops:
  12.4 22.2 %all-to-all-start.1 = ((bf16[4,768,256]{2,1,0:T(8,128)(2,1)}), bf16[4,768,256]{2,1,0:T(8,128)(2,1)S(1)}, u32[]{:S(2)}, u32[]{:S(2)}) async-start(bf16[4,768,256]{2,1,0:T(8,128)(2,1)} %broadcast_in_dim.41), calls=%async_computation.1 | async-start | bytes 3145728 | tf_op jit(solution)/shard_map/all_to_all | solution.py:19
  34.6 68.6 %copy-start.1 = (s32[768]{0:T(1024)S(1)}, s32[768]{0:T(1024)}, u32[]{:S(2)}) copy-start(s32[768]{0:T(1024)} %param.12) | copy-start | bytes 9220
  34.6 5.1 %copy-start = (s32[8192]{0:T(1024)S(1)}, s32[8192]{0:T(1024)}, u32[]{:S(2)}) copy-start(s32[8192]{0:T(1024)} %get-tuple-element.151) | copy-start | bytes 98308 | tf_op jit(solution)/shard_map/while
  44.5 5.1 %copy-start = (s32[8192]{0:T(1024)S(1)}, s32[8192]{0:T(1024)}, u32[]{:S(2)}) copy-start(s32[8192]{0:T(1024)} %get-tuple-element.151) | copy-start | bytes 98308 | tf_op jit(solution)/shard_map/while
  54.5 5.1 %copy-start = (s32[8192]{0:T(1024)S(1)}, s32[8192]{0:T(1024)}, u32[]{:S(2)}) copy-start(s32[8192]{0:T(1024)} %get-tuple-element.151) | copy-start | bytes 98308 | tf_op jit(solution)/shard_map/while
  64.4 5.1 %copy-start = (s32[8192]{0:T(1024)S(1)}, s32[8192]{0:T(1024)}, u32[]{:S(2)}) copy-start(s32[8192]{0:T(1024)} %get-tuple-element.151) | copy-start | bytes 98308 | tf_op jit(solution)/shard_map/while
  74.3 5.1 %copy-start = (s32[8192]{0:T(1024)S(1)}, s32[8192]{0:T(1024)}, u32[]{:S(2)}) copy-start(s32[8192]{0:T(1024)} %get-tuple-element.151) | copy-start | bytes 98308 | tf_op jit(solution)/shard_map/while
  84.2 5.1 %copy-start = (s32[8192]{0:T(1024)S(1)}, s32[8192]{0:T(1024)}, u32[]{:S(2)}) copy-start(s32[8192]{0:T(1024)} %get-tuple-element.151) | copy-start | bytes 98308 | tf_op jit(solution)/shard_map/while
  94.9 7.9 %all-to-all-start.2 = ((f32[4,2,3072]{2,1,0:T(2,128)}), f32[4,2,3072]{2,1,0:T(2,128)S(1)}, u32[]{:S(2)}, u32[]{:S(2)}) async-start(f32[4,2,3072]{2,1,0:T(2,128)} %broadcast_in_dim.42), calls=%async_computation.2 | async-start | bytes 196608 | tf_op jit(solution)/shard_map/all_to_all | solution.py:19
where the time goes:
time: 155 us; the launch traced here: 154 us
  blocking collectives  55.3 us (36%)
  other arithmetic  31.3 us (20%)
  matrix products  30.5 us (20%)
  waiting for transfers between devices  19.8 us (13%)
  starting transfers between devices  6.86 us (4%)
  local copies, waits for them, and re-layouts  6.69 us (4%)
  between operations  3.14 us (2%)
    psum x4, blocking collectives, one_axis_at_a_time(): return functools.reduce(lax.psum, axes, array)  46.5 us
    dot_general x6, matrix products, shard_partials(): lax.dot_general(rows, columns, (((1,), (1,)), ((), ())), preferred_elemen...  30.5 us
    reduce_sum x6, other arithmetic, shard_partials(): jnp.sum(jnp.where(hit, 0.0, jnp.exp(logits - peak[:, None])), axis=1)  27.9 us
    all_to_all x2, waiting for transfers between devices, copy_for_each(): lax.all_to_all(jnp.broadcast_to(array[None], (peers, *array.shape)), axis...  19.8 us
    all_to_all x1, blocking collectives, copy_for_each(): lax.all_to_all(jnp.broadcast_to(array[None], (peers, *array.shape)), axis...  8.81 us
    all_to_all x2, starting transfers between devices, copy_for_each(): lax.all_to_all(jnp.broadcast_to(array[None], (peers, *array.shape)), axis...  6.86 us
    broadcast_in_dim x3, local copies, waits for them, and re-layouts, copy_for_each(): jnp.broadcast_to(array[None], (peers, *array.shape))  3.59 us
  transfers between devices with their start and end apart: 2, of which 2 were waited for; matrix products, arithmetic and copies ran while one was open for 2% of the time, Pallas kernels for 0%

commit v1 on v0

v1 whole, which is shorter than its diff:
```python
import functools
import math

import jax
import jax.numpy as jnp
from jax import lax
from jax.experimental import pallas as pl
from jax.experimental.pallas import tpu as pltpu
from jax.sharding import PartitionSpec as P

MESH = pl.DeviceIdType.MESH
LOG2E = math.log2(math.e)
LN2 = math.log(2.0)
MASKED = -1e30
FLOOR = -1e20
NEG = 4
TILES = 3
STEPS = NEG * TILES
FROM_LEFT = {0: 3, 1: 5, 2: 7}
FROM_RIGHT = {2: 4, 1: 6, 0: 8}
FROM_FAR = {0: 9, 2: 10, 1: 11}


def nt_dot(a, b):
    return lax.dot_general(a, b, (((1,), (1,)), ((), ())), preferred_element_type=jnp.float32)


def kernel(
    dims, chunk, scale2,
    user, positive, row_ids, weights, offsets, neg, neg_ids,
    loss_out, mean_out,
    rows_v, ids_v, pos_v, neg_v, nid_v, bufs, part, got, sum_a, sum_b,
    load_sem, row_send, fwd_send, row_recv, id_send, id_recv, part_send, part_recv,
    a_send, a_recv, b_send, b_recv,
):
    ny, nz, nc = dims
    per_y = nz * nc
    n = lax.axis_index("neg")
    d = lax.axis_index("dp")
    y, inner = d // per_y, d % per_y
    z, core = inner // nc, inner % nc
    right, left, far = (n + 1) % NEG, (n + 3) % NEG, (n + 2) % NEG
    tile = rows_v.shape[0] // STEPS
    half = tile // 2
    halves = tile // 128
    tokens = TILES * tile
    negs = neg_v.shape[0]
    number = negs // chunk
    group = chunk // 8

    peers_a = [
        (k, ((y + k // NEG) % ny) * per_y + inner, (n + k % NEG) % NEG) for k in range(1, ny * NEG)
    ]
    peers_b = [
        (k, y * per_y + ((z + k // nc) % nz) * nc + (core + k % nc) % nc, n)
        for k in range(1, per_y)
    ]

    own = rows_v.at[pl.ds(0, tokens), :]
    loads = [
        pltpu.make_async_copy(user, own, load_sem.at[0]),
        pltpu.make_async_copy(row_ids, ids_v.at[pl.ds(0, TILES)], load_sem.at[1]),
        pltpu.make_async_copy(neg, neg_v, load_sem.at[2]),
        pltpu.make_async_copy(positive, pos_v, load_sem.at[3]),
    ]
    for load in loads:
        load.start()

    barrier = pltpu.get_barrier_semaphore()
    for _, dp_to, neg_to in peers_a + peers_b:
        pl.semaphore_signal(barrier, inc=1, device_id=(dp_to, neg_to), device_id_type=MESH)

    for r in range(negs // 128):
        nid_v[r * 128 : (r + 1) * 128, :] = jnp.broadcast_to(
            neg_ids[r : r + 1, :], (128, 128)
        ).T
    for load in loads[:2]:
        load.wait()
    pl.semaphore_wait(barrier, len(peers_a) + len(peers_b))

    def rows_at(step, start=0, size=None):
        return rows_v.at[pl.ds(step * tile + start, size or tile), :]

    def remote(src, dst, send, recv, to):
        return pltpu.make_async_remote_copy(
            src_ref=src, dst_ref=dst, send_sem=send, recv_sem=recv,
            device_id=(d, to), device_id_type=MESH,
        )

    def id_copy(index, j, step, to):
        return remote(ids_v.at[j], ids_v.at[step], id_send.at[index], id_recv.at[step], to)

    def row_copy(index, j, step, to):
        return remote(rows_at(j), rows_at(step), row_send.at[index], row_recv.at[step], to)

    id_copies, row_copies = [], []
    for j in range(TILES):
        for table, to in ((FROM_LEFT, right), (FROM_RIGHT, left), (FROM_FAR, far)):
            id_copies.append(id_copy(len(id_copies), j, table[j], to))
    for jr, jl in ((0, 2), (1, 1), (2, 0)):
        row_copies.append(row_copy(len(row_copies), jr, FROM_LEFT[jr], right))
        row_copies.append(row_copy(len(row_copies), jl, FROM_RIGHT[jl], left))
    for copy in id_copies + row_copies:
        copy.start()

    forward = [
        remote(rows_at(3), rows_at(9), fwd_send.at[0], row_recv.at[9], right),
        remote(rows_at(4), rows_at(10), fwd_send.at[1], row_recv.at[10], left),
        remote(rows_at(5, 0, half), rows_at(11, 0, half), fwd_send.at[2], row_recv.at[11], right),
        remote(
            rows_at(6, half, half), rows_at(11, half, half), fwd_send.at[3], row_recv.at[12], left
        ),
    ]
    loads[2].wait()

    def one_tile(s, carry):
        @pl.when(jnp.logical_and(s >= 3, s < 11))
        def _():
            remote(rows_at(0), rows_at(s), row_send.at[0], row_recv.at[s], right).wait_recv()

        @pl.when(s >= 3)
        def _():
            remote(ids_v.at[0], ids_v.at[s], id_send.at[0], id_recv.at[s], right).wait_recv()

        @pl.when(s == 11)
        def _():
            forward[2].wait_recv()
            forward[3].wait_recv()

        @pl.when(s == 4)
        def _():
            forward[0].start()
            forward[1].start()

        @pl.when(s == 6)
        def _():
            forward[2].start()
            forward[3].start()

        u = rows_v.at[pl.ds(pl.multiple_of(s * tile, tile), tile), :]
        rid = [ids_v[s, :, h * 128 : (h + 1) * 128] for h in range(halves)]

        def front(c):
            logits = nt_dot(neg_v[c * chunk : (c + 1) * chunk, :], u[...])
            peaks = []
            for h in range(halves):
                x = logits[:, h * 128 : (h + 1) * 128] * scale2
                x = jnp.where(nid_v[c * chunk : (c + 1) * chunk, :] == rid[h], MASKED, x)
                bufs[c % 2, :, h * 128 : (h + 1) * 128] = x
                peaks.append(jnp.max(x.reshape(group, 8, 128), axis=0))
            return peaks

        def back(state, peaks, c):
            out = []
            for h in range(halves):
                peak, total = state[h]
                new = jnp.maximum(peak, peaks[h])
                x = bufs[c % 2, :, h * 128 : (h + 1) * 128].reshape(group // 4, 4, 8, 128)
                e = jnp.sum(jnp.exp2(x - new[None, None]), axis=0)
                out.append((new, total * jnp.exp2(peak - new) + jnp.sum(e, axis=0)))
            return out

        state = [
            (jnp.full((8, 128), FLOOR, jnp.float32), jnp.zeros((8, 128), jnp.float32))
            for _ in range(halves)
        ]
        peaks = front(0)
        for c in range(number):
            later = front(c + 1) if c + 1 < number else None
            state = back(state, peaks, c)
            peaks = later
        for h, (peak, total) in enumerate(state):
            top = jnp.max(peak, axis=0, keepdims=True)
            total = jnp.sum(total * jnp.exp2(peak - top), axis=0, keepdims=True)
            value = jnp.where(total > 0.0, top + jnp.log2(jnp.maximum(total, 1e-37)), MASKED)
            part[s, :, h * 128 : (h + 1) * 128] = value
        return carry

    lax.fori_loop(0, STEPS, one_tile, 0)

    part_copies = []
    for slot, table, to in ((3, FROM_FAR, far), (1, FROM_LEFT, left), (2, FROM_RIGHT, right)):
        for j in range(TILES):
            index = len(part_copies)
            part_copies.append(
                remote(part.at[table[j]], got.at[slot, j], part_send.at[index],
                       part_recv.at[index], to)
            )
    for copy in part_copies:
        copy.start()

    loads[3].wait()
    ones = jnp.ones((8, rows_v.shape[1]), jnp.bfloat16)
    lane = lax.broadcasted_iota(jnp.int32, (1, tile), 1)
    ready = []
    for j in range(TILES):
        product = rows_v[j * tile : (j + 1) * tile, :].astype(jnp.float32) * pos_v[
            j * tile : (j + 1) * tile, :
        ].astype(jnp.float32)
        high = product.astype(jnp.bfloat16)
        low = (product - high.astype(jnp.float32)).astype(jnp.bfloat16)
        pos2 = (nt_dot(ones, high) + nt_dot(ones, low))[0:1, :] * scale2
        place = n * tokens + j * tile + lane
        live = place < offsets[0, offsets.shape[1] - 1]
        for k in range(1, offsets.shape[1]):
            live = jnp.logical_and(live, place + 1 != offsets[0, k])
        ready.append((pos2, live, weights[j].astype(jnp.float32)))

    for copy in part_copies:
        copy.wait_recv()
    total = jnp.zeros((1, 128), jnp.float32)
    count = jnp.zeros((1, 128), jnp.float32)
    for j, (pos2, live, weight) in enumerate(ready):
        terms = [pos2, part[j], got[1, j], got[2, j], got[3, j]]
        top = functools.reduce(jnp.maximum, terms)
        summed = functools.reduce(jnp.add, [jnp.exp2(term - top) for term in terms])
        loss = jnp.where(live, (top - pos2 + jnp.log2(summed)) * LN2, 0.0)
        loss_out[j] = loss
        weighted = weight * loss
        counted = jnp.where(live, weight, 0.0)
        for h in range(halves):
            total = total + weighted[:, h * 128 : (h + 1) * 128]
            count = count + counted[:, h * 128 : (h + 1) * 128]

    def exchange(buffer, mine, peers, send, recv):
        copies = [
            pltpu.make_async_remote_copy(
                src_ref=buffer.at[mine], dst_ref=buffer.at[mine], send_sem=send.at[k],
                recv_sem=recv.at[k], device_id=(dp_to, neg_to), device_id_type=MESH,
            )
            for k, dp_to, neg_to in peers
        ]
        for copy in copies:
            copy.start()
        return copies

    def summed_slots(buffer):
        parts = [buffer[k] for k in range(buffer.shape[0])]
        while len(parts) > 1:
            parts = [a + b for a, b in zip(parts[::2], parts[1::2])]
        return parts[0]

    slot_a = y * NEG + n
    sum_a[slot_a, 0:1, :] = total
    sum_a[slot_a, 1:2, :] = count
    copies_a = exchange(sum_a, slot_a, peers_a, a_send, a_recv)
    for copy in copies_a:
        copy.wait_recv()
    sum_b[inner] = summed_slots(sum_a)
    copies_b = exchange(sum_b, inner, peers_b, b_send, b_recv)
    for copy in row_copies + id_copies + forward + part_copies + copies_a:
        copy.wait_send()
    for copy in copies_b:
        copy.wait_recv()
    both = summed_slots(sum_b)
    mean_out[...] = jnp.sum(both[0:1, :], axis=1, keepdims=True) / jnp.sum(
        both[1:2, :], axis=1, keepdims=True
    )
    for copy in copies_b:
        copy.wait_send()


def build(dims, chunk):
    def shards(user, positive, row_ids, weights, offsets, neg, neg_ids):
        tokens, width = user.shape
        negs = neg.shape[0]
        tile = tokens // TILES
        ny, nz, nc = dims
        size_a, size_b = ny * NEG, nz * nc
        in_any = pl.BlockSpec(memory_space=pl.ANY)
        in_vmem = pl.BlockSpec(memory_space=pltpu.VMEM)
        dma = pltpu.SemaphoreType.DMA
        f32, bf16, i32 = jnp.float32, jnp.bfloat16, jnp.int32
        flops = 2 * NEG * tokens * negs * width
        loss, mean = pl.pallas_call(
            functools.partial(kernel, dims, chunk, 3.0 / math.sqrt(width) * LOG2E),
            out_shape=(
                jax.ShapeDtypeStruct((TILES, 1, tile), f32),
                jax.ShapeDtypeStruct((1, 1), f32),
            ),
            in_specs=[
                in_any, in_any, in_vmem, in_vmem, pl.BlockSpec(memory_space=pltpu.SMEM),
                in_any, in_vmem,
            ],
            out_specs=(in_vmem, in_vmem),
            scratch_shapes=[
                pltpu.VMEM((STEPS * tile, width), bf16),
                pltpu.VMEM((STEPS, 1, tile), i32),
                pltpu.VMEM((tokens, width), bf16),
                pltpu.VMEM((negs, width), bf16),
                pltpu.VMEM((negs, 128), i32),
                pltpu.VMEM((2, chunk, tile), f32),
                pltpu.VMEM((STEPS, 1, tile), f32),
                pltpu.VMEM((NEG, TILES, 1, tile), f32),
                pltpu.VMEM((size_a, 2, 128), f32),
                pltpu.VMEM((size_b, 2, 128), f32),
                dma((4,)), dma((6,)), dma((4,)), dma((13,)), dma((9,)), dma((12,)),
                dma((9,)), dma((9,)),
                dma((size_a,)), dma((size_a,)), dma((size_b,)), dma((size_b,)),
            ],
            compiler_params=pltpu.CompilerParams(
                collective_id=0, has_side_effects=True, vmem_limit_bytes=48 * 2**20
            ),
            cost_estimate=pl.CostEstimate(
                flops=flops, bytes_accessed=2 * negs * width, transcendentals=0
            ),
        )(
            user, positive, row_ids.reshape(TILES, 1, tile), weights.reshape(TILES, 1, tile),
            offsets, neg, neg_ids.reshape(negs // 128, 128),
        )
        return loss.reshape(tokens), mean.reshape(())

    return shards


def on_mesh(mesh, dims, chunk):
    both = ("dp", "neg")
    return jax.shard_map(
        build(dims, chunk),
        mesh=mesh,
        in_specs=(
            P(both, None), P(both, None), P(both), P(both), P("dp", None),
            P("neg", None), P("neg"),
        ),
        out_specs=(P(both), P()),
        check_vma=False,
    )


def solution(mesh):
    return on_mesh(mesh, (4, 8, 2), 512)
```

time: 155 us -> 69.3 us (0.45)
  Pallas kernels: 0 us -> 59 us
  blocking collectives: 55.3 us -> 0 us
  other arithmetic: 31.3 us -> 0.02 us
  matrix products: 30.5 us -> 0 us
  waiting for transfers between devices: 19.8 us -> 0 us
  starting transfers between devices: 6.86 us -> 0 us
    pallas_call x0 -> x1, Pallas kernels: none -> 59 us  [shards(): pl.pallas_call(functools.partial(kernel, dims, chunk, 3.0 / math.sqrt(wid...]
    psum x4 -> x0, blocking collectives: 46.5 us -> none  [one_axis_at_a_time(): return functools.reduce(lax.psum, axes, array)]
    reduce_sum x8 -> x0, other arithmetic: 31 us -> none  [the longest x6 27.9 us: shard_partials(): jnp.sum(jnp.where(hit, 0.0, jnp.exp(logits - peak[:, None])), axis=1)]
    dot_general x6 -> x0, matrix products: 30.5 us -> none  [shard_partials(): lax.dot_general(rows, columns, (((1,), (1,)), ((), ())), preferred_elemen...]
    all_to_all x2 -> x0, waiting for transfers between devices: 19.8 us -> none  [copy_for_each(): lax.all_to_all(jnp.broadcast_to(array[None], (peers, *array.shape)), axis...]
    all_to_all x1 -> x0, blocking collectives: 8.81 us -> none  [copy_for_each(): lax.all_to_all(jnp.broadcast_to(array[None], (peers, *array.shape)), axis...]
    all_to_all x2 -> x0, starting transfers between devices: 6.86 us -> none  [copy_for_each(): lax.all_to_all(jnp.broadcast_to(array[None], (peers, *array.shape)), axis...]
    unnamed x4 -> x10, local copies, waits for them, and re-layouts: 0.03 us -> 5.59 us
  transfers between devices with their start and end apart: 2 -> 0, of which waited for: 2 -> 0; matrix products, arithmetic and copies ran while one was open for 2% -> 0% of each run, Pallas kernels for 0% -> 0%
where the time goes in v1:
time: 69.3 us; the launch traced here: 69 us
  Pallas kernels  59 us (85%)
  local copies, waits for them, and re-layouts  7.58 us (11%)
  between operations  2.38 us (3%)
    pallas_call x1, Pallas kernels, shards(): pl.pallas_call(functools.partial(kernel, dims, chunk, 3.0 / math.sqrt(wid...  59 us
    unnamed x10, local copies, waits for them, and re-layouts  5.59 us

profile of v1, /device:TPU:1, one launch (start us, length us, event | category | flops | bytes accessed | tf_op | source)
XLA Modules:
  0.0 69.0 jit_solution(8984328533808051213)
XLA Ops:
  0.6 0.7 %reshape.19.row_ids = s32[3,1,256]{2,1,0:T(1,128)S(1)} reshape(s32[768]{0:T(1024)} %param.9) | data formatting | bytes 6144 | tf_op jit(solution)/shard_map/reshape | solution.py:308
  1.3 0.7 %reshape.20.weights = s32[3,1,256]{2,1,0:T(1,128)S(1)} reshape(s32[768]{0:T(1024)} %param.10) | data formatting | bytes 6144 | tf_op jit(solution)/shard_map/reshape | solution.py:308
  2.0 0.0 copy-start
  2.0 2.2 %copy-done = bf16[8192,256]{1,0:T(8,128)(2,1)S(1)} copy-done((bf16[8192,256]{1,0:T(8,128)(2,1)S(1)}, bf16[8192,256]{1,0:T(8,128)(2,1)}, u32[]{:S(2)}) %copy-start) | copy-done | bytes 4194328
  4.2 0.0 copy-start.1
  4.2 1.0 %copy-done.1 = bf16[768,256]{1,0:T(8,128)(2,1)S(1)} copy-done((bf16[768,256]{1,0:T(8,128)(2,1)S(1)}, bf16[768,256]{1,0:T(8,128)(2,1)}, u32[]{:S(2)}) %copy-start.1) | copy-done | bytes 393240
  5.2 0.0 copy-start.2
  5.2 1.0 %copy-done.2 = bf16[768,256]{1,0:T(8,128)(2,1)S(1)} copy-done((bf16[768,256]{1,0:T(8,128)(2,1)S(1)}, bf16[768,256]{1,0:T(8,128)(2,1)}, u32[]{:S(2)}) %copy-start.2) | copy-done | bytes 393240
  6.2 0.0 copy-start.3
  6.2 0.8 %copy-done.3 = s32[8192]{0:T(1024)S(1)} copy-done((s32[8192]{0:T(1024)S(1)}, s32[8192]{0:T(1024)}, u32[]{:S(2)}) %copy-start.3) | copy-done | bytes 32792
  7.0 0.0 copy-start.4
  7.0 0.7 copy-done.4
  7.6 59.0 %shard_map.86 = (f32[3,1,256]{2,1,0:T(1,128)S(1)}, f32[1,1]{1,0:T(1,128)}) custom-call(bf16[768,256]{1,0:T(8,128)(2,1)S(1)} %copy-done.1, bf16[768,256]{1,0:T(8,128)(2,1)S(1)} %copy-done.2, s32[3,1,256]{2,1,0:T(1,128)S(1)} %reshape.19.row_ids, s32[3,1,256]{2,1,0:T(1,128)S(1)} %reshape.20.weights, s32[1,25]{1,0:T(1,128)S(1)} %copy-done.4, ...), custom_call_target="tpu_custom_call" | custom-call | flops 12884901888 | bytes 4194304 | tf_op jit(solution)/shard_map/pallas_call | solution.py:275
  66.6 0.6 reshape.22
  (1 shorter events, 0.0 us)
Async XLA Ops:
  2.0 2.2 %copy-start = (bf16[8192,256]{1,0:T(8,128)(2,1)S(1)}, bf16[8192,256]{1,0:T(8,128)(2,1)}, u32[]{:S(2)}) copy-start(bf16[8192,256]{1,0:T(8,128)(2,1)} %neg.1) | copy-start | bytes 12582916
  4.2 1.0 %copy-start.1 = (bf16[768,256]{1,0:T(8,128)(2,1)S(1)}, bf16[768,256]{1,0:T(8,128)(2,1)}, u32[]{:S(2)}) copy-start(bf16[768,256]{1,0:T(8,128)(2,1)} %user.1) | copy-start | bytes 1179652
  5.2 1.0 %copy-start.2 = (bf16[768,256]{1,0:T(8,128)(2,1)S(1)}, bf16[768,256]{1,0:T(8,128)(2,1)}, u32[]{:S(2)}) copy-start(bf16[768,256]{1,0:T(8,128)(2,1)} %positive.1) | copy-start | bytes 1179652
  6.2 0.8 %copy-start.3 = (s32[8192]{0:T(1024)S(1)}, s32[8192]{0:T(1024)}, u32[]{:S(2)}) copy-start(s32[8192]{0:T(1024)} %param.13) | copy-start | bytes 98308
  7.0 0.7 copy-start.4

commit v2 on v1

--- a/solution.py
+++ b/solution.py
@@ -30,6 +30,7 @@
     user, positive, row_ids, weights, offsets, neg, neg_ids,
     loss_out, mean_out,
     rows_v, ids_v, pos_v, neg_v, nid_v, bufs, part, got, sum_a, sum_b,
+    id_rows, weight_rows, nid_rows, ends,
     load_sem, row_send, fwd_send, row_recv, id_send, id_recv, part_send, part_recv,
     a_send, a_recv, b_send, b_recv,
 ):
@@ -57,11 +58,12 @@
     ]
 
     own = rows_v.at[pl.ds(0, tokens), :]
+    pairs = (
+        (neg_ids, nid_rows), (row_ids, id_rows), (user, own), (neg, neg_v),
+        (positive, pos_v), (weights, weight_rows), (offsets, ends),
+    )
     loads = [
-        pltpu.make_async_copy(user, own, load_sem.at[0]),
-        pltpu.make_async_copy(row_ids, ids_v.at[pl.ds(0, TILES)], load_sem.at[1]),
-        pltpu.make_async_copy(neg, neg_v, load_sem.at[2]),
-        pltpu.make_async_copy(positive, pos_v, load_sem.at[3]),
+        pltpu.make_async_copy(src, dst, load_sem.at[k]) for k, (src, dst) in enumerate(pairs)
     ]
     for load in loads:
         load.start()
@@ -70,12 +72,17 @@
     for _, dp_to, neg_to in peers_a + peers_b:
         pl.semaphore_signal(barrier, inc=1, device_id=(dp_to, neg_to), device_id_type=MESH)
 
+    loads[0].wait()
+    loads[1].wait()
+    for j in range(TILES):
+        for h in range(halves):
+            row = j * halves + h
+            ids_v[j, :, h * 128 : (h + 1) * 128] = id_rows[row : row + 1, :]
     for r in range(negs // 128):
         nid_v[r * 128 : (r + 1) * 128, :] = jnp.broadcast_to(
-            neg_ids[r : r + 1, :], (128, 128)
+            nid_rows[r : r + 1, :], (128, 128)
         ).T
-    for load in loads[:2]:
-        load.wait()
+    loads[2].wait()
     pl.semaphore_wait(barrier, len(peers_a) + len(peers_b))
 
     def rows_at(step, start=0, size=None):
@@ -111,7 +118,7 @@
             rows_at(6, half, half), rows_at(11, half, half), fwd_send.at[3], row_recv.at[12], left
         ),
     ]
-    loads[2].wait()
+    loads[3].wait()
 
     def one_tile(s, carry):
         @pl.when(jnp.logical_and(s >= 3, s < 11))
@@ -189,7 +196,8 @@
     for copy in part_copies:
         copy.start()
 
-    loads[3].wait()
+    for load in loads[4:]:
+        load.wait()
     ones = jnp.ones((8, rows_v.shape[1]), jnp.bfloat16)
     lane = lax.broadcasted_iota(jnp.int32, (1, tile), 1)
     ready = []
@@ -201,26 +209,27 @@
         low = (product - high.astype(jnp.float32)).astype(jnp.bfloat16)
         pos2 = (nt_dot(ones, high) + nt_dot(ones, low))[0:1, :] * scale2
         place = n * tokens + j * tile + lane
-        live = place < offsets[0, offsets.shape[1] - 1]
-        for k in range(1, offsets.shape[1]):
-            live = jnp.logical_and(live, place + 1 != offsets[0, k])
-        ready.append((pos2, live, weights[j].astype(jnp.float32)))
+        live = place < ends[0, ends.shape[1] - 1]
+        for k in range(1, ends.shape[1]):
+            live = jnp.logical_and(live, place + 1 != ends[0, k])
+        ready.append((pos2, live))
 
     for copy in part_copies:
         copy.wait_recv()
     total = jnp.zeros((1, 128), jnp.float32)
     count = jnp.zeros((1, 128), jnp.float32)
-    for j, (pos2, live, weight) in enumerate(ready):
+    for j, (pos2, live) in enumerate(ready):
         terms = [pos2, part[j], got[1, j], got[2, j], got[3, j]]
         top = functools.reduce(jnp.maximum, terms)
         summed = functools.reduce(jnp.add, [jnp.exp2(term - top) for term in terms])
         loss = jnp.where(live, (top - pos2 + jnp.log2(summed)) * LN2, 0.0)
-        loss_out[j] = loss
-        weighted = weight * loss
-        counted = jnp.where(live, weight, 0.0)
+        alive = jnp.where(live, 1.0, 0.0)
         for h in range(halves):
-            total = total + weighted[:, h * 128 : (h + 1) * 128]
-            count = count + counted[:, h * 128 : (h + 1) * 128]
+            row = j * halves + h
+            weight = weight_rows[row : row + 1, :].astype(jnp.float32)
+            loss_out[row : row + 1, :] = loss[:, h * 128 : (h + 1) * 128]
+            total = total + weight * loss[:, h * 128 : (h + 1) * 128]
+            count = count + weight * alive[:, h * 128 : (h + 1) * 128]
 
     def exchange(buffer, mine, peers, send, recv):
         copies = [
@@ -264,7 +273,7 @@
     def shards(user, positive, row_ids, weights, offsets, neg, neg_ids):
         tokens, width = user.shape
         negs = neg.shape[0]
-        tile = tokens // TILES
+        tile, lines = tokens // TILES, tokens // 128
         ny, nz, nc = dims
         size_a, size_b = ny * NEG, nz * nc
         in_any = pl.BlockSpec(memory_space=pl.ANY)
@@ -275,13 +284,10 @@
         loss, mean = pl.pallas_call(
             functools.partial(kernel, dims, chunk, 3.0 / math.sqrt(width) * LOG2E),
             out_shape=(
-                jax.ShapeDtypeStruct((TILES, 1, tile), f32),
+                jax.ShapeDtypeStruct((lines, 128), f32),
                 jax.ShapeDtypeStruct((1, 1), f32),
             ),
-            in_specs=[
-                in_any, in_any, in_vmem, in_vmem, pl.BlockSpec(memory_space=pltpu.SMEM),
-                in_any, in_vmem,
-            ],
+            in_specs=[in_any] * 7,
             out_specs=(in_vmem, in_vmem),
             scratch_shapes=[
                 pltpu.VMEM((STEPS * tile, width), bf16),
@@ -294,18 +300,22 @@
                 pltpu.VMEM((NEG, TILES, 1, tile), f32),
                 pltpu.VMEM((size_a, 2, 128), f32),
                 pltpu.VMEM((size_b, 2, 128), f32),
-                dma((4,)), dma((6,)), dma((4,)), dma((13,)), dma((9,)), dma((12,)),
+                pltpu.VMEM((lines, 128), i32),
+                pltpu.VMEM((lines, 128), i32),
+                pltpu.VMEM((negs // 128, 128), i32),
+                pltpu.SMEM(offsets.shape, i32),
+                dma((7,)), dma((6,)), dma((4,)), dma((13,)), dma((9,)), dma((12,)),
                 dma((9,)), dma((9,)),
                 dma((size_a,)), dma((size_a,)), dma((size_b,)), dma((size_b,)),
             ],
             compiler_params=pltpu.CompilerParams(
-                collective_id=0, has_side_effects=True, vmem_limit_bytes=48 * 2**20
+                collective_id=0, has_side_effects=True
             ),
             cost_estimate=pl.CostEstimate(
                 flops=flops, bytes_accessed=2 * negs * width, transcendentals=0
             ),
         )(
-            user, positive, row_ids.reshape(TILES, 1, tile), weights.reshape(TILES, 1, tile),
+            user, positive, row_ids.reshape(lines, 128), weights.reshape(lines, 128),
             offsets, neg, neg_ids.reshape(negs // 128, 128),
         )
         return loss.reshape(tokens), mean.reshape(())
@@ -328,4 +338,4 @@
 
 
 def solution(mesh):
-    return on_mesh(mesh, (4, 8, 2), 512)
+    return on_mesh(mesh, (4, 8, 2), 256)

time: 69.3 us -> 62.1 us (0.90)
  local copies, waits for them, and re-layouts: 7.58 us -> 1.26 us
  Pallas kernels: 59 us -> 58.2 us
    unnamed x10 -> x1, local copies, waits for them, and re-layouts: 5.59 us -> 1.26 us
    reshape x3 -> x0, local copies, waits for them, and re-layouts: 1.99 us -> none  [the longest x1 0.7 us: shards(): row_ids.reshape(TILES, 1, tile)]
    pallas_call x1, Pallas kernels: 59 us -> 58.2 us  [shards(): pl.pallas_call(functools.partial(kernel, dims, chunk, 3.0 / math.sqrt(wid...]
where the time goes in v2:
time: 62.1 us; the launch traced here: 61.9 us
  Pallas kernels  58.2 us (94%)
  between operations  2.4 us (4%)
  local copies, waits for them, and re-layouts  1.26 us (2%)
    pallas_call x1, Pallas kernels, shards(): pl.pallas_call(functools.partial(kernel, dims, chunk, 3.0 / math.sqrt(wid...  58.2 us
    unnamed x1, local copies, waits for them, and re-layouts  1.26 us

profile of v2, /device:TPU:1, one launch (start us, length us, event | category | flops | bytes accessed | tf_op | source)
XLA Modules:
  0.0 61.9 jit_solution(522287627609637029)
XLA Ops:
  0.6 58.2 %shard_map.86 = (f32[6,128]{1,0:T(8,128)}, f32[1,1]{1,0:T(1,128)}) custom-call(bf16[768,256]{1,0:T(8,128)(2,1)} %user.1, bf16[768,256]{1,0:T(8,128)(2,1)} %positive.1, s32[6,128]{1,0:T(8,128)} %bitcast.7, s32[6,128]{1,0:T(8,128)} %bitcast.8, s32[1,25]{1,0:T(1,128)} %offsets.1, bf16[8192,256]{1,0:T(8,128)(2,1)} %neg.1, s32[64,128]{1,0:T(8,128)} %bitcast.6), custom_call_target="tpu_custom_call" | custom-call | flops 12884901888 | bytes 4194304 | tf_op jit(solution)/shard_map/pallas_call | solution.py:284
  58.9 1.3 %copy.11 = f32[768]{0:T(1024)} copy(f32[768]{0:T(1024)} %bitcast.5) | data formatting | bytes 6144
